TPU v7x, 32 devices: a whole 2x2x4 slice. The times are simulated.
32 devices in a mesh: gx: 4 (over z), gy: 4 (over y, x), gz: 2 (over core).
Axes of the slice: x: 2, y: 2, z: 4, core: 2. Of those that a mesh axis runs over, the one named last changes fastest.
Arguments:
- metric: float32 [6, 64, 64, 256], P(None, 'gx', 'gy', 'gz'), may hold values from -1 to 9
- curvature: float32 [6, 64, 64, 256], P(None, 'gx', 'gy', 'gz'), may hold values from -1.8 to 1.8
- conserved: float32 [4, 64, 64, 256], P(None, 'gx', 'gy', 'gz'), may hold values from -0.3 to 1, as said below
- matter_mask: int32 [4, 4, 16], P('gx', 'gy', 'gz'), may hold values from 0 to 1, as said below
Outputs:
- metric_next: float32 [6, 64, 64, 256], P(None, 'gx', 'gy', 'gz')
- curvature_next: float32 [6, 64, 64, 256], P(None, 'gx', 'gy', 'gz')
- conserved_next: float32 [4, 64, 64, 256], P(None, 'gx', 'gy', 'gz')
Inputs may be any that keep to these rules, and one draw needn't show every extreme that they name: `conserved`: component 0 is the density, from 0.25 to 1; components 1 to 3 are the momentum. `matter_mask`: 1 marks a matter-bearing meshblock of 16 x 16 x 16 cells.
All inputs are finite; a program needn't handle non-finite values.
Results may differ from a plain program's by a relative error of at most 0.00002.
Values sent between devices are 32-bit elements; how exact they have to be, the bound alone decides.
A program may use at most 64 MiB of HBM per device.

v0:
```python
import math

import jax
import jax.numpy as jnp
from jax import lax
from jax.sharding import PartitionSpec as P

MB = 16


second_stencil = (1.0 / 90.0, -3.0 / 20.0, 1.5, -49.0 / 18.0, 1.5, -3.0 / 20.0, 1.0 / 90.0)
first_stencil = (-1.0 / 60.0, 3.0 / 20.0, -0.75, 0.0, 0.75, -3.0 / 20.0, 1.0 / 60.0)
sound_square = 0.25
sound_speed = 0.5
courant = 0.3
eight_pi = 8.0 * math.pi
pair_first = (0, 0, 0, 1, 1, 2)
pair_second = (0, 1, 2, 1, 2, 2)


def extended(value, sides, width):
    for axis, dim in sides:
        peers, length = (lax.axis_size(axis), value.shape[dim])
        up = [(i, (i + 1) % peers) for i in range(peers)]
        down = [(j, i) for i, j in up]
        last = lax.slice_in_dim(value, length - width, length, axis=dim)
        first = lax.slice_in_dim(value, 0, width, axis=dim)
        before = lax.ppermute(last, axis, up)
        after = lax.ppermute(first, axis, down)
        value = jnp.concatenate([before, value, after], axis=dim)
    return value


def expand_mask(matter_mask, block_edge):
    blocks_x, blocks_y, blocks_z = matter_mask.shape
    spread = jnp.broadcast_to(
        matter_mask[:, None, :, None, :, None],
        (blocks_x, block_edge, blocks_y, block_edge, blocks_z, block_edge),
    )
    return spread.reshape(blocks_x * block_edge, blocks_y * block_edge, blocks_z * block_edge) > 0


def shifted(padded, margin, extent, direction, offset):
    starts = [margin, margin, margin]
    starts[direction] = starts[direction] + offset
    return padded[
        :,
        starts[0] : starts[0] + extent[0],
        starts[1] : starts[1] + extent[1],
        starts[2] : starts[2] + extent[2],
    ]


def strip_along(padded, margin, extent, direction):
    starts = [margin, margin, margin]
    stops = [margin + extent[0], margin + extent[1], margin + extent[2]]
    starts[direction] = starts[direction] - 1
    stops[direction] = stops[direction] + 1
    return padded[:, starts[0] : stops[0], starts[1] : stops[1], starts[2] : stops[2]]


def stencil_sum(padded, margin, extent, stencil, direction):
    total = jnp.zeros((padded.shape[0],) + tuple(extent), jnp.float32)
    for offset in range(-3, 4):
        if stencil[offset + 3] != 0.0:
            total = total + stencil[offset + 3] * shifted(padded, margin, extent, direction, offset)
    return total


def advance_fluid(fluid_padded, potential_padded, extent, speed_max, step):
    center = shifted(fluid_padded, 1, extent, 0, 0)
    density = center[0]
    divergence = jnp.zeros_like(center)
    for direction in range(3):
        strip = strip_along(fluid_padded, 1, extent, direction)
        strip_density = strip[0]
        strip_moment = strip[1:4]
        velocity = strip_moment[direction] / strip_density
        flux_moment = strip_moment * velocity[None]
        flux_moment = flux_moment.at[direction].add(sound_square * strip_density)
        flux = jnp.concatenate([strip_moment[direction][None], flux_moment], axis=0)
        length = strip.shape[direction + 1]
        lower_flux = lax.slice_in_dim(flux, 0, length - 1, axis=direction + 1)
        upper_flux = lax.slice_in_dim(flux, 1, length, axis=direction + 1)
        lower_state = lax.slice_in_dim(strip, 0, length - 1, axis=direction + 1)
        upper_state = lax.slice_in_dim(strip, 1, length, axis=direction + 1)
        face = 0.5 * (lower_flux + upper_flux) - 0.5 * speed_max * (upper_state - lower_state)
        faces = length - 1
        divergence = divergence + (
            lax.slice_in_dim(face, 1, faces, axis=direction + 1)
            - lax.slice_in_dim(face, 0, faces - 1, axis=direction + 1)
        )
    gradient = jnp.concatenate(
        [
            stencil_sum(potential_padded, 3, extent, first_stencil, direction)
            for direction in range(3)
        ],
        axis=0,
    )
    source = jnp.concatenate([jnp.zeros_like(density)[None], density[None] * gradient], axis=0)
    return center - step * divergence + step * source


def body(metric, curvature, conserved, matter_mask):
    extent = (metric.shape[1], metric.shape[2], metric.shape[3])
    cell_mask = expand_mask(matter_mask, MB)
    density = conserved[0]
    moment = conserved[1:4]
    speed = jnp.max(jnp.abs(moment), axis=0) / density + sound_speed
    local_speed = jnp.max(jnp.where(cell_mask, speed, jnp.float32(sound_speed)))
    speed_max = lax.pmax(local_speed, ("gx", "gy", "gz"))
    step = courant / speed_max
    stacked = jnp.concatenate([metric, conserved], axis=0)
    padded_all = extended(stacked, (("gx", 1), ("gy", 2), ("gz", 3)), 3)
    metric_padded = padded_all[:6]
    fluid_padded = padded_all[6:, 2:-2, 2:-2, 2:-2]
    laplacian = stencil_sum(metric_padded, 3, extent, second_stencil, 0)
    laplacian = laplacian + stencil_sum(metric_padded, 3, extent, second_stencil, 1)
    laplacian = laplacian + stencil_sum(metric_padded, 3, extent, second_stencil, 2)
    stress_list = []
    for component in range(6):
        first = pair_first[component]
        second = pair_second[component]
        term = moment[first] * moment[second] / density
        if first == second:
            term = term + sound_square * density
        stress_list.append(term)
    stress = jnp.stack(stress_list)
    curvature_next = curvature + step * (eight_pi * stress - 0.5 * laplacian)
    metric_next = metric - 2.0 * step * curvature
    potential_padded = 0.5 * (metric_padded[0:1] + metric_padded[3:4] + metric_padded[5:6])
    advanced = advance_fluid(fluid_padded, potential_padded, extent, speed_max, step)
    conserved_next = jnp.where(cell_mask[None], advanced, conserved)
    return (metric_next, curvature_next, conserved_next)


def solution(mesh):
    in_specs = (
        P(None, "gx", "gy", "gz"),
        P(None, "gx", "gy", "gz"),
        P(None, "gx", "gy", "gz"),
        P("gx", "gy", "gz"),
    )
    out_specs = (P(None, "gx", "gy", "gz"), P(None, "gx", "gy", "gz"), P(None, "gx", "gy", "gz"))
    return jax.shard_map(body, mesh=mesh, in_specs=in_specs, out_specs=out_specs, check_vma=False)
```

profile of v0, /device:TPU:0, one launch (start us, length us, event | category | flops | bytes accessed | tf_op | source)
XLA Modules:
  0.0 120.5 jit_solution(11277265745976096150)
XLA Ops:
  0.6 0.0 copy-start.2
  0.6 1.1 abs_reduce_fusion
  1.7 0.7 compare_bitcast_fusion
  2.4 0.1 broadcast_in_dim.24
  2.5 0.1 broadcast_in_dim.25
  2.6 1.6 %select_reduce_fusion = f32[]{:T(128)} fusion(f32[16,16,128]{2,1,0:T(8,128)S(1)} %abs_reduce_fusion, pred[128]{0:T(512)(128)(4,1)S(1)} %broadcast_in_dim.25, f32[4,16,16,128]{3,2,1,0:T(8,128)} %param.12), kind=kLoop, calls=%fused_computation.176 | loop fusion | flops 131071 | bytes 262276 | tf_op jit(solution)/shard_map/reduce_max | solution.py:110
  4.1 42.2 %pmax.7 = f32[]{:T(128)} all-reduce(f32[]{:T(128)} %select_reduce_fusion), channel_id=1, replica_groups=mesh['gx'=4,'gy'=4,'gz'=2] {'gx','gy','gz'}, use_global_device_ids=true, to_apply=%region_2.3 | all-reduce | flops 1 | bytes 8 | tf_op jit(solution)/shard_map/pmax | solution.py:111
  47.0 2.4 %constant_dynamic-update-slice_fusion.1 = (f32[10,16,16,128]{3,2,1,0:T(8,128)S(1)}, f32[6,16,16,128]{3,2,1,0:T(8,128)}) fusion(f32[6,16,16,128]{3,2,1,0:T(8,128)} %param.10, f32[6,16,16,128]{3,2,1,0:T(8,128)} %param.11, f32[]{:T(128)S(6)} %mul_shard_map.3), kind=kLoop, calls=%fused_computation.179 | loop fusion | flops 393215 | bytes 3145732
  49.4 0.0 copy-done.2
  49.4 0.8 fusion.81
  50.2 2.2 %collective-permute-start.1 = (f32[10,3,16,128]{3,2,1,0:T(8,128)}, f32[10,3,16,128]{3,2,1,0:T(8,128)S(1)}, u32[]{:S(2)}, u32[]{:S(2)}) collective-permute-start(f32[10,3,16,128]{3,2,1,0:T(8,128)} %get-tuple-element.58), channel_id=1, source_target_pairs={{8,0},{16,8},{24,16},{0,24},{9,1},{17,9},{25,17},{1,25},{10,2},{18... | collective-permute-start | bytes 737288 | tf_op jit(solution)/shard_map/ppermute | solution.py:29
  52.4 0.0 collective-permute-start
  53.3 0.0 copy-start.11
  53.3 5.8 %collective-permute-done.1 = f32[10,3,16,128]{3,2,1,0:T(8,128)S(1)} collective-permute-done((f32[10,3,16,128]{3,2,1,0:T(8,128)}, f32[10,3,16,128]{3,2,1,0:T(8,128)S(1)}, u32[]{:S(2)}, u32[]{:S(2)}) %collective-permute-start.1) | collective-permute-done | bytes 245792 | tf_op jit(solution)/shard_map/ppermute | solution.py:29
  59.1 5.5 %collective-permute-done = f32[10,3,16,128]{3,2,1,0:T(8,128)S(1)} collective-permute-done((f32[10,3,16,128]{3,2,1,0:T(8,128)}, f32[10,3,16,128]{3,2,1,0:T(8,128)S(1)}, u32[]{:S(2)}, u32[]{:S(2)}) %collective-permute-start) | collective-permute-done | bytes 245792 | tf_op jit(solution)/shard_map/ppermute | solution.py:28
  64.5 0.2 pad_maximum_fusion.2
  64.7 0.2 fusion.80
  64.9 0.0 copy-done.11
  64.9 2.3 %collective-permute-start.3 = (f32[10,22,3,128]{3,1,2,0:T(8,128)S(1)}, f32[10,22,3,128]{3,1,2,0:T(8,128)S(1)}, u32[]{:S(2)}, u32[]{:S(2)}) collective-permute-start(f32[10,22,3,128]{3,1,2,0:T(8,128)S(1)} %copy.27), channel_id=1, source_target_pairs={{2,0},{4,2},{6,4},{0,6},{3,1},{5,3},{7,5},{1,7},{10,8},{12,10},{14... | collective-permute-start | bytes 1013768 | tf_op jit(solution)/shard_map/ppermute | solution.py:29
  67.3 0.1 collective-permute-start.2
  67.4 0.1 fusion.61
  67.5 0.9 fusion.48
  68.4 8.0 %collective-permute-done.3 = f32[10,22,3,128]{3,1,2,0:T(8,128)S(1)} collective-permute-done((f32[10,22,3,128]{3,1,2,0:T(8,128)S(1)}, f32[10,22,3,128]{3,1,2,0:T(8,128)S(1)}, u32[]{:S(2)}, u32[]{:S(2)}) %collective-permute-start.3) | collective-permute-done | bytes 337952 | tf_op jit(solution)/shard_map/ppermute | solution.py:29
  76.4 0.1 copy.28
  76.6 5.5 %collective-permute-done.2 = f32[10,22,3,128]{3,1,2,0:T(8,128)S(1)} collective-permute-done((f32[10,22,3,128]{3,1,2,0:T(8,128)S(1)}, f32[10,22,3,128]{3,1,2,0:T(8,128)S(1)}, u32[]{:S(2)}, u32[]{:S(2)}) %collective-permute-start.2) | collective-permute-done | bytes 337952 | tf_op jit(solution)/shard_map/ppermute | solution.py:28
  82.1 0.1 copy.26
  82.2 0.4 pad_maximum_fusion.1
  82.6 3.2 %fusion.79 = (f32[10,22,22,3]{3,2,1,0:T(8,128)}, f32[10,22,22,3]{3,2,1,0:T(8,128)}) fusion(f32[10,22,22,128]{3,2,1,0:T(8,128)S(1)} %pad_maximum_fusion.1), kind=kLoop, calls=%fused_computation.181 | loop fusion | bytes 232320 | tf_op jit(solution)/shard_map/slice | solution.py:26
  85.9 4.0 %copy.33 = f32[10,22,22,3]{2,1,3,0:T(8,128)} copy(f32[10,22,22,3]{3,2,1,0:T(8,128)} %get-tuple-element.52) | data formatting | bytes 116160 | tf_op jit(solution)/shard_map/slice | solution.py:27
  89.9 0.0 collective-permute-start.5
  89.9 4.1 %copy.31 = f32[10,22,22,3]{2,1,3,0:T(8,128)} copy(f32[10,22,22,3]{3,2,1,0:T(8,128)} %get-tuple-element.51) | data formatting | bytes 116160 | tf_op jit(solution)/shard_map/slice | solution.py:26
  93.9 0.5 collective-permute-start.4
  94.4 0.1 divide_bitcast_fusion.1
  94.5 0.1 maximum_multiply_fusion.7
  94.7 0.7 maximum_maximum_fusion
  95.4 0.0 copy-start.3
  95.4 0.0 copy-start.5
  95.4 1.5 %copy-done.3 = f32[10,22,19,128]{3,2,1,0:T(8,128)} copy-done((f32[10,22,19,128]{3,2,1,0:T(8,128)}, f32[10,22,19,128]{3,2,1,0:T(8,128)S(1)}, u32[]{:S(2)}) %copy-start.3) | copy-done | bytes 2140184
  96.9 1.1 fusion.30
  98.1 0.0 collective-permute-done.5
  98.1 3.9 %copy.34 = f32[10,22,22,3]{3,2,1,0:T(8,128)} copy(f32[10,22,22,3]{2,1,3,0:T(8,128)} %collective-permute-done.5) | data formatting | bytes 116160 | tf_op jit(solution)/shard_map/ppermute | solution.py:29
  102.0 0.0 collective-permute-done.4
  102.0 4.0 %copy.32 = f32[10,22,22,3]{3,2,1,0:T(8,128)} copy(f32[10,22,22,3]{2,1,3,0:T(8,128)} %collective-permute-done.4) | data formatting | bytes 116160 | tf_op jit(solution)/shard_map/ppermute | solution.py:28
  106.0 2.5 %fusion.52 = f32[1,22,22,134]{3,2,1,0:T(8,128)S(1)} fusion(f32[10,22,22,3]{3,2,1,0:T(8,128)} %copy.34, f32[10,22,22,3]{3,2,1,0:T(8,128)} %copy.32, f32[10,22,3,128]{3,2,1,0:T(4,128)S(1)} %copy.28, f32[10,22,3,128]{3,2,1,0:T(4,128)S(1)} %copy.26, f32[10,3,16,128]{3,2,1,0:T(8,128)S(1)} %collective-permute-done.1, ...), kind=kLoop, calls=%fused_computation.102 | loop fusion | flops 1361976 | bytes 2853664 | tf_op jit(solution)/shard_map/mul | solution.py:131
  108.5 0.0 copy-start
  108.5 0.6 fusion.74
  109.2 0.0 copy-done.1
  109.2 1.1 copy-done
  110.3 0.4 divide_bitcast_fusion
  110.7 0.6 maximum_multiply_fusion
  111.3 0.1 fusion.59
  111.4 0.0 copy-start.7
  111.4 0.0 copy-start.8
  111.4 0.0 copy-start.6
  111.4 0.0 copy-start.12
  111.4 0.9 fusion.2
  112.4 0.1 copy-done.7
  112.5 0.3 copy-done.8
  112.7 1.1 fusion.57
  113.8 0.0 copy-done.6
  113.8 1.2 %copy-done.4 = f32[10,22,19,128]{3,2,1,0:T(8,128)S(1)} copy-done((f32[10,22,19,128]{3,2,1,0:T(8,128)S(1)}, f32[10,22,19,128]{3,2,1,0:T(8,128)}, u32[]{:S(2)}) %copy-start.4) | copy-done | bytes 2140184
  115.1 0.1 copy-done.9
  115.2 0.2 copy-done.10
  115.4 5.0 %fusion.13 = f32[6,16,16,128]{3,2,1,0:T(8,128)} fusion(f32[6,16,16,128]{3,2,1,0:T(8,128)S(1)} %copy-done.10, f32[10,16,16,128]{3,2,1,0:T(8,128)S(1)} %constant_dynamic-update-slice_fusion, f32[10,3,16,128]{3,2,1,0:T(8,128)S(1)} %collective-permute-done.1, f32[10,3,16,128]{3,2,1,0:T(8,128)S(1)} %collective-permute-done, f32[10,22,22,3]{3,2,1,0:T(8,128)S(1)} %copy-done, ...), kind=kLoop, calls=%fused_computation.40 | loop fusion | flops 15728640 | bytes 10458564 | tf_op jit(solution)/shard_map/add | solution.py:129
  (19 shorter events, 0.4 us)
Async XLA Ops:
  0.6 48.7 %copy-start.2 = (f32[4,16,16,128]{3,2,1,0:T(8,128)S(1)}, f32[4,16,16,128]{3,2,1,0:T(8,128)}, u32[]{:S(2)}) copy-start(f32[4,16,16,128]{3,2,1,0:T(8,128)} %param.12) | copy-start | bytes 1572868
  50.2 8.9 %collective-permute-start.1 = (f32[10,3,16,128]{3,2,1,0:T(8,128)}, f32[10,3,16,128]{3,2,1,0:T(8,128)S(1)}, u32[]{:S(2)}, u32[]{:S(2)}) collective-permute-start(f32[10,3,16,128]{3,2,1,0:T(8,128)} %get-tuple-element.58), channel_id=1, source_target_pairs={{8,0},{16,8},{24,16},{0,24},{9,1},{17,9},{25,17},{1,25},{10,2},{18... | collective-permute-start | bytes 737288 | tf_op jit(solution)/shard_map/ppermute | solution.py:29
  52.4 12.1 %collective-permute-start = (f32[10,3,16,128]{3,2,1,0:T(8,128)}, f32[10,3,16,128]{3,2,1,0:T(8,128)S(1)}, u32[]{:S(2)}, u32[]{:S(2)}) collective-permute-start(f32[10,3,16,128]{3,2,1,0:T(8,128)} %get-tuple-element.57), channel_id=1, source_target_pairs={{0,8},{8,16},{16,24},{24,0},{1,9},{9,17},{17,25},{25,1},{2,10},{10... | collective-permute-start | bytes 737288 | tf_op jit(solution)/shard_map/ppermute | solution.py:28
  53.3 11.6 %copy-start.11 = (f32[6,16,16,128]{3,2,1,0:T(8,128)}, f32[6,16,16,128]{3,2,1,0:T(8,128)S(1)}, u32[]{:S(2)}) copy-start(f32[6,16,16,128]{3,2,1,0:T(8,128)S(1)} %add_dynamic-update-slice_fusion) | copy-start | bytes 2359300
  64.9 11.5 %collective-permute-start.3 = (f32[10,22,3,128]{3,1,2,0:T(8,128)S(1)}, f32[10,22,3,128]{3,1,2,0:T(8,128)S(1)}, u32[]{:S(2)}, u32[]{:S(2)}) collective-permute-start(f32[10,22,3,128]{3,1,2,0:T(8,128)S(1)} %copy.27), channel_id=1, source_target_pairs={{2,0},{4,2},{6,4},{0,6},{3,1},{5,3},{7,5},{1,7},{10,8},{12,10},{14... | collective-permute-start | bytes 1013768 | tf_op jit(solution)/shard_map/ppermute | solution.py:29
  67.3 14.8 %collective-permute-start.2 = (f32[10,22,3,128]{3,1,2,0:T(8,128)S(1)}, f32[10,22,3,128]{3,1,2,0:T(8,128)S(1)}, u32[]{:S(2)}, u32[]{:S(2)}) collective-permute-start(f32[10,22,3,128]{3,1,2,0:T(8,128)S(1)} %copy.25), channel_id=1, source_target_pairs={{0,2},{2,4},{4,6},{6,0},{1,3},{3,5},{5,7},{7,1},{8,10},{10,12},{12... | collective-permute-start | bytes 1013768 | tf_op jit(solution)/shard_map/ppermute | solution.py:28
  89.9 8.2 %collective-permute-start.5 = (f32[10,22,22,3]{2,1,3,0:T(8,128)}, f32[10,22,22,3]{2,1,3,0:T(8,128)}, u32[]{:S(2)}, u32[]{:S(2)}) collective-permute-start(f32[10,22,22,3]{2,1,3,0:T(8,128)} %copy.33), channel_id=1, source_target_pairs={{1,0},{0,1},{3,2},{2,3},{5,4},{4,5},{7,6},{6,7},{9,8},{8,9},{11,10... | collective-permute-start | bytes 174248 | tf_op jit(solution)/shard_map/ppermute | solution.py:29
  93.9 8.1 %collective-permute-start.4 = (f32[10,22,22,3]{2,1,3,0:T(8,128)}, f32[10,22,22,3]{2,1,3,0:T(8,128)}, u32[]{:S(2)}, u32[]{:S(2)}) collective-permute-start(f32[10,22,22,3]{2,1,3,0:T(8,128)} %copy.31), channel_id=1, source_target_pairs={{0,1},{1,0},{2,3},{3,2},{4,5},{5,4},{6,7},{7,6},{8,9},{9,8},{10,11... | collective-permute-start | bytes 174248 | tf_op jit(solution)/shard_map/ppermute | solution.py:28
  95.4 1.5 %copy-start.3 = (f32[10,22,19,128]{3,2,1,0:T(8,128)}, f32[10,22,19,128]{3,2,1,0:T(8,128)S(1)}, u32[]{:S(2)}) copy-start(f32[10,22,19,128]{3,2,1,0:T(8,128)S(1)} %get-tuple-element.53) | copy-start | bytes 6420484
  95.4 2.7 %copy-start.5 = (f32[10,22,19,128]{3,2,1,0:T(8,128)}, f32[10,22,19,128]{3,2,1,0:T(8,128)S(1)}, u32[]{:S(2)}) copy-start(f32[10,22,19,128]{3,2,1,0:T(8,128)S(1)} %get-tuple-element.54) | copy-start | bytes 6420484
  106.0 3.2 %copy-start.1 = (f32[10,22,22,3]{3,2,1,0:T(8,128)S(1)}, f32[10,22,22,3]{3,2,1,0:T(8,128)}, u32[]{:S(2)}) copy-start(f32[10,22,22,3]{3,2,1,0:T(8,128)} %copy.32) | copy-start | bytes 174244
  108.5 1.8 %copy-start = (f32[10,22,22,3]{3,2,1,0:T(8,128)S(1)}, f32[10,22,22,3]{3,2,1,0:T(8,128)}, u32[]{:S(2)}) copy-start(f32[10,22,22,3]{3,2,1,0:T(8,128)} %copy.34) | copy-start | bytes 174244
  111.4 1.1 copy-start.7
  111.4 1.3 %copy-start.8 = (f32[4,16,17,128]{3,2,1,0:T(8,128)S(1)}, f32[4,16,17,128]{3,2,1,0:T(8,128)}, u32[]{:S(2)}) copy-start(f32[4,16,17,128]{3,2,1,0:T(8,128)} %fusion.30) | copy-start | bytes 1671172
  111.4 2.4 %copy-start.6 = (f32[10,22,19,128]{3,2,1,0:T(8,128)S(1)}, f32[10,22,19,128]{3,2,1,0:T(8,128)}, u32[]{:S(2)}) copy-start(f32[10,22,19,128]{3,2,1,0:T(8,128)} %copy-done.5) | copy-start | bytes 6420484
  111.4 2.4 %copy-start.12 = (f32[6,16,16,128]{3,2,1,0:T(8,128)S(1)}, f32[6,16,16,128]{3,2,1,0:T(8,128)}, u32[]{:S(2)}) copy-start(f32[6,16,16,128]{3,2,1,0:T(8,128)} %copy-done.11) | copy-start | bytes 2359300
  112.7 2.3 %copy-start.4 = (f32[10,22,19,128]{3,2,1,0:T(8,128)S(1)}, f32[10,22,19,128]{3,2,1,0:T(8,128)}, u32[]{:S(2)}) copy-start(f32[10,22,19,128]{3,2,1,0:T(8,128)} %copy-done.3) | copy-start | bytes 6420484
  112.7 2.5 %copy-start.9 = (f32[6,16,16,128]{3,2,1,0:T(8,128)S(1)}, f32[6,16,16,128]{3,2,1,0:T(8,128)}, u32[]{:S(2)}) copy-start(f32[6,16,16,128]{3,2,1,0:T(8,128)} %param.10) | copy-start | bytes 2359300
  112.7 2.7 %copy-start.10 = (f32[6,16,16,128]{3,2,1,0:T(8,128)S(1)}, f32[6,16,16,128]{3,2,1,0:T(8,128)}, u32[]{:S(2)}) copy-start(f32[6,16,16,128]{3,2,1,0:T(8,128)} %param.11) | copy-start | bytes 2359300
where the time goes:
time: 121 us; the launch traced here: 120 us
  blocking collectives  42.2 us (35%)
  local copies, waits for them, and re-layouts  25.2 us (21%)
  waiting for transfers between devices  24.8 us (20%)
  other arithmetic  20.9 us (17%)
  starting transfers between devices  5.1 us (4%)
  between operations  2.26 us (2%)
    pmax x1, blocking collectives, body(): speed_max = lax.pmax(local_speed, ('gx', 'gy', 'gz'))  42.2 us
    ppermute x3, waiting for transfers between devices, extended(): after = lax.ppermute(first, axis, down)  13.8 us
    ppermute x3, waiting for transfers between devices, extended(): before = lax.ppermute(last, axis, up)  11 us
    slice x5, local copies, waits for them, and re-layouts, extended(): last = lax.slice_in_dim(value, length - width, length, axis=dim)  8.28 us
    add x1, other arithmetic, body(): curvature_next = curvature + step * (eight_pi * stress - 0.5 * laplacian)  5.05 us
    unnamed x26, local copies, waits for them, and re-layouts  4.55 us
    ppermute x3, starting transfers between devices, extended(): after = lax.ppermute(first, axis, down)  4.53 us
    ppermute x2, local copies, waits for them, and re-layouts, extended(): before = lax.ppermute(last, axis, up)  4.12 us
  transfers between devices with their start and end apart: 6, of which 4 were waited for; matrix products, arithmetic and copies ran while one was open for 9% of the time, Pallas kernels for 0%

commit v1 on v0

v1 whole, which is shorter than its diff:
```python
import functools
import math

import jax
import jax.numpy as jnp
from jax import lax
from jax.experimental import pallas as pl
from jax.experimental.pallas import tpu as pltpu
from jax.sharding import PartitionSpec as P

MESH = pl.DeviceIdType.MESH
AXES = ("gx", "gy", "gz")
MB = 16
second = (-49.0 / 18.0, 1.5, -3.0 / 20.0, 1.0 / 90.0)
first = (0.0, 0.75, -3.0 / 20.0, 1.0 / 60.0)
sound_square = 0.25
sound_speed = 0.5
courant = 0.3
eight_pi = 8.0 * math.pi
pair_first = (0, 0, 0, 1, 1, 2)
pair_second = (0, 1, 2, 1, 2, 2)
trace_part = (0, 3, 5)
W = 3
SUB = 8


def peer(sizes, axes, offset):
    position = 0
    for axis in axes:
        position = position * sizes[axis] + lax.axis_index(axis)
    total = math.prod(sizes[axis] for axis in axes)
    position = lax.rem(position + offset, total)
    found = {}
    for axis in reversed(axes):
        found[axis] = lax.rem(position, sizes[axis])
        position = position // sizes[axis]
    return {axis: found.get(axis, lax.axis_index(axis)) for axis in AXES}


def stages_of(sizes):
    if math.prod(sizes.values()) <= 64:
        return (AXES,)
    return (("gz",), ("gy",), ("gx",))


def flux_of(state, direction):
    density, moment = state[0], state[1:]
    velocity = moment[direction] / density
    flux = [moment[direction]] + [moment[i] * velocity for i in range(3)]
    flux[1 + direction] = flux[1 + direction] + sound_square * density
    return flux


def kernel(sizes, shape, metric_hbm, fluid_hbm, mask_ref, curv_out, fluid_out, step_out,
           mp, up, ez, uz, ey, uy, acc_c, acc_f, acc_l, row, *rest):
    nx, ny, nz = shape
    stages = stages_of(sizes)
    bufs = rest[: len(stages)]
    load_sem, send_sem, recv_sem, row_send, row_recv = rest[len(stages):]
    tiles = ny // SUB

    own_m = mp.at[:, pl.ds(W, nx)]
    own_u = up.at[:, pl.ds(1, nx)]
    load_u = pltpu.make_async_copy(fluid_hbm, own_u, load_sem.at[0])
    load_m = pltpu.make_async_copy(metric_hbm, own_m, load_sem.at[1])
    load_u.start()
    load_m.start()

    barrier = pltpu.get_barrier_semaphore()
    greeted = 0
    for axes in stages:
        total = math.prod(sizes[axis] for axis in axes)

        def greet(j, carry, axes=axes):
            pl.semaphore_signal(barrier, inc=1, device_id=peer(sizes, axes, j), device_id_type=MESH)
            return carry

        lax.fori_loop(1, total, greet, 0)
        greeted += total - 1

    lane = lax.broadcasted_iota(jnp.int32, (ny, nz), 1)
    block = lane // MB
    mask = jnp.zeros((ny, nz), jnp.int32)
    for b in range(nz // MB):
        mask = jnp.where(block == b, mask_ref[0, 0, b], mask)
    mask = mask > 0

    load_u.wait()

    def local_speed(x, best):
        moment = jnp.maximum(jnp.maximum(jnp.abs(up[1, x + 1]), jnp.abs(up[2, x + 1])), jnp.abs(up[3, x + 1]))
        speed = moment / up[0, x + 1] + sound_speed
        return jnp.maximum(best, jnp.where(mask, speed, jnp.float32(sound_speed)))

    best = lax.fori_loop(0, nx, local_speed, jnp.full((ny, nz), sound_speed, jnp.float32), unroll=4)
    best = jnp.max(best, axis=0, keepdims=True)
    row[0] = best
    load_m.wait()
    pl.semaphore_wait(barrier, greeted)

    def spread(index):
        axes = stages[index]
        total = math.prod(sizes[axis] for axis in axes)

        def send(j, carry):
            pltpu.make_async_remote_copy(
                src_ref=row.at[index], dst_ref=bufs[index].at[j - 1],
                send_sem=row_send.at[index], recv_sem=row_recv.at[index],
                device_id=peer(sizes, axes, j), device_id_type=MESH,
            ).start()
            return carry

        lax.fori_loop(1, total, send, 0)

    def gathered(index, best):
        buf = bufs[index]
        pltpu.make_async_copy(buf, buf, row_recv.at[index]).wait()
        pltpu.make_async_copy(buf, buf, row_send.at[index]).wait()
        return jnp.maximum(best, jnp.max(buf[...], axis=0))

    spread(0)

    count = [0]

    def remote(src, dst, axis, offset):
        n = count[0]
        count[0] += 1
        copy = pltpu.make_async_remote_copy(
            src_ref=src, dst_ref=dst, send_sem=send_sem.at[n], recv_sem=recv_sem.at[n],
            device_id=peer(sizes, (axis,), offset % sizes[axis]), device_id_type=MESH,
        )
        copy.start()
        return copy

    y_copies = [
        remote(mp.at[:, pl.ds(W, nx), pl.ds(ny - W, W)], ey.at[:, :, pl.ds(SUB - W, W)], "gy", 1),
        remote(mp.at[:, pl.ds(W, nx), pl.ds(0, W)], ey.at[:, :, pl.ds(0, W)], "gy", -1),
        remote(up.at[:, pl.ds(1, nx), pl.ds(ny - 1, 1)], uy.at[:, :, pl.ds(SUB - 1, 1)], "gy", 1),
        remote(up.at[:, pl.ds(1, nx), pl.ds(0, 1)], uy.at[:, :, pl.ds(0, 1)], "gy", -1),
    ]
    x_copies = [
        remote(mp.at[:, pl.ds(nx, W)], mp.at[:, pl.ds(0, W)], "gx", 1),
        remote(mp.at[:, pl.ds(W, W)], mp.at[:, pl.ds(nx + W, W)], "gx", -1),
        remote(up.at[:, pl.ds(nx, 1)], up.at[:, pl.ds(0, 1)], "gx", 1),
        remote(up.at[:, pl.ds(1, 1)], up.at[:, pl.ds(nx + 1, 1)], "gx", -1),
    ]
    z_copies = [remote(own_u, uz.at[0], "gz", -1), remote(own_m, ez.at[0], "gz", -1)]
    if sizes["gz"] > 2:
        z_copies += [remote(own_u, uz.at[1], "gz", 1), remote(own_m, ez.at[1], "gz", 1)]

    def edge(ref, c, x):
        if sizes["gz"] > 2:
            return jnp.where(lane < nz // 2, ref[0, c, x], ref[1, c, x])
        return ref[0, c, x]

    def z_up(own, other, k):
        return pltpu.roll(jnp.where(lane < k, other, own), nz - k, 1)

    def z_down(own, other, k):
        return pltpu.roll(jnp.where(lane >= nz - k, other, own), k, 1)

    sub = lax.broadcasted_iota(jnp.int32, (SUB, nz), 0)

    def cut(value):
        return [value[t * SUB : (t + 1) * SUB] for t in range(tiles)]

    def y_pair(value, k):
        own = cut(value)
        zero = jnp.zeros_like(own[0])
        after = own[1:] + [zero]
        before = [zero] + own[:-1]
        up_rows = [pltpu.roll(jnp.where(sub < k, after[t], own[t]), SUB - k, 0) for t in range(tiles)]
        down_rows = [pltpu.roll(jnp.where(sub >= SUB - k, before[t], own[t]), k, 0) for t in range(tiles)]
        return jnp.concatenate(up_rows, axis=0), jnp.concatenate(down_rows, axis=0)

    for copy in z_copies:
        copy.wait()

    def inner(x, carry):
        state = [up[c, x + 1] for c in range(4)]
        density, moment = state[0], state[1:]
        other = [edge(uz, c, x) for c in range(4)]
        above = [z_up(state[c], other[c], 1) for c in range(4)]
        below = [z_down(state[c], other[c], 1) for c in range(4)]
        flux_above, flux_below = flux_of(above, 2), flux_of(below, 2)
        flux_y = flux_of(state, 1)
        slopes = []
        for c in range(4):
            y_above, y_below = y_pair(state[c], 1)
            fy_above, fy_below = y_pair(flux_y[c], 1)
            slopes.append((flux_above[c] - flux_below[c]) + (fy_above - fy_below))
            acc_l[c, x] = (above[c] + below[c]) + (y_above + y_below) - 6.0 * state[c]
        grad_y = jnp.zeros((ny, nz), jnp.float32)
        grad_z = jnp.zeros((ny, nz), jnp.float32)
        inverse = 1.0 / density
        for c in range(6):
            own = mp[c, x + W]
            far = edge(ez, c, x)
            total = (3.0 * second[0]) * own
            for k in range(1, W + 1):
                zu, zd = z_up(own, far, k), z_down(own, far, k)
                yu, yd = y_pair(own, k)
                total = total + second[k] * ((zu + zd) + (yu + yd))
                if c in trace_part:
                    grad_z = grad_z + first[k] * (zu - zd)
                    grad_y = grad_y + first[k] * (yu - yd)
            stress = moment[pair_first[c]] * (moment[pair_second[c]] * inverse)
            if pair_first[c] == pair_second[c]:
                stress = stress + sound_square * density
            acc_c[c, x] = eight_pi * stress - 0.5 * total
        acc_f[0, x] = -0.5 * slopes[0]
        acc_f[1, x] = -0.5 * slopes[1]
        acc_f[2, x] = -0.5 * slopes[2] + (0.5 * density) * grad_y
        acc_f[3, x] = -0.5 * slopes[3] + (0.5 * density) * grad_z
        return carry

    lax.fori_loop(0, nx, inner, 0)

    for copy in x_copies:
        copy.wait()

    def along_x(x, carry):
        above = [up[c, x + 2] for c in range(4)]
        below = [up[c, x] for c in range(4)]
        flux_above, flux_below = flux_of(above, 0), flux_of(below, 0)
        grad = jnp.zeros((ny, nz), jnp.float32)
        for c in range(6):
            total = jnp.zeros((ny, nz), jnp.float32)
            for k in range(1, W + 1):
                high, low = mp[c, x + W + k], mp[c, x + W - k]
                total = total + second[k] * (high + low)
                if c in trace_part:
                    grad = grad + first[k] * (high - low)
            acc_c[c, x] = acc_c[c, x] - 0.5 * total
        for c in range(4):
            value = acc_f[c, x] - 0.5 * (flux_above[c] - flux_below[c])
            if c == 1:
                value = value + (0.5 * up[0, x + 1]) * grad
            acc_f[c, x] = value
            acc_l[c, x] = acc_l[c, x] + (above[c] + below[c])
        return carry

    lax.fori_loop(0, nx, along_x, 0)

    best = gathered(0, best)
    for index in range(1, len(stages)):
        row[index] = best
        spread(index)
        best = gathered(index, best)
    speed_max = jnp.max(best, axis=1, keepdims=True)
    step = courant / speed_max
    step_out[...] = jnp.broadcast_to(step, step_out.shape)
    step_all = jnp.broadcast_to(step, (ny, nz))
    half_speed = jnp.broadcast_to(0.5 * speed_max, (ny, nz))

    for copy in y_copies:
        copy.wait()

    inside = jnp.logical_and(sub >= W, sub < SUB - W)
    weight, slope = [None], [None]
    for k in range(1, W + 1):
        touched = jnp.where(jnp.logical_or(sub < k, sub >= SUB - k), 1.0, 0.0)
        weight.append(touched * jnp.float32(second[k]))
        slope.append(jnp.where(sub < SUB // 2, -1.0, 1.0) * touched * jnp.float32(first[k]))
    low_half = sub < SUB // 2
    nothing = jnp.zeros((SUB, nz), jnp.float32)

    def placed(value):
        parts = [jnp.where(low_half, value, nothing)] + [nothing] * (tiles - 2) + [jnp.where(low_half, nothing, value)]
        return jnp.concatenate(parts, axis=0)

    def finish(x, carry):
        grad = nothing
        for c in range(6):
            halo = jnp.where(inside, nothing, ey[c, x])
            total = nothing
            for k in range(1, W + 1):
                near = jnp.where(low_half, pltpu.roll(halo, k, 0), pltpu.roll(halo, SUB - k, 0))
                total = total + weight[k] * near
                if c in trace_part:
                    grad = grad + slope[k] * near
            curv_out[c, x] = step_all * (acc_c[c, x] - 0.5 * placed(total))
        halo = [uy[c, x] for c in range(4)]
        flux = flux_of(halo, 1)
        density = up[0, x + 1]
        for c in range(4):
            near = jnp.where(sub == 0, pltpu.roll(halo[c], 1, 0), pltpu.roll(halo[c], SUB - 1, 0))
            near_flux = jnp.where(sub == 0, -pltpu.roll(flux[c], 1, 0), pltpu.roll(flux[c], SUB - 1, 0))
            end = jnp.logical_or(sub == 0, sub == SUB - 1)
            near = placed(jnp.where(end, near, nothing))
            near_flux = placed(jnp.where(end, near_flux, nothing))
            value = acc_f[c, x] - 0.5 * near_flux
            if c == 2:
                value = value + (0.5 * density) * placed(grad)
            value = step_all * (value + half_speed * (acc_l[c, x] + near))
            fluid_out[c, x] = jnp.where(mask, value, 0.0)
        return carry

    lax.fori_loop(0, nx, finish, 0)


def body(sizes, metric, curvature, conserved, matter_mask):
    shape = metric.shape[1:]
    nx, ny, nz = shape
    assert matter_mask.shape[:2] == (1, 1) and ny % SUB == 0 and ny >= 2 * SUB
    stages = stages_of(sizes)
    totals = [math.prod(sizes[axis] for axis in axes) for axes in stages]
    sides = 2 if sizes["gz"] > 2 else 1
    copies = 8 + 2 * sides
    vmem, sem = pltpu.VMEM, pltpu.SemaphoreType.DMA
    f32 = jnp.float32
    curv_add, fluid_add, step = pl.pallas_call(
        functools.partial(kernel, sizes, shape),
        out_shape=(
            jax.ShapeDtypeStruct((6,) + shape, f32),
            jax.ShapeDtypeStruct((4,) + shape, f32),
            jax.ShapeDtypeStruct((SUB, nz), f32),
        ),
        in_specs=[
            pl.BlockSpec(memory_space=pl.ANY),
            pl.BlockSpec(memory_space=pl.ANY),
            pl.BlockSpec(memory_space=pltpu.SMEM),
        ],
        out_specs=(pl.BlockSpec(memory_space=vmem),) * 3,
        scratch_shapes=[
            vmem((6, nx + 2 * W, ny, nz), f32),
            vmem((4, nx + 2, ny, nz), f32),
            vmem((sides, 6, nx, ny, nz), f32),
            vmem((sides, 4, nx, ny, nz), f32),
            vmem((6, nx, SUB, nz), f32),
            vmem((4, nx, SUB, nz), f32),
            vmem((6, nx, ny, nz), f32),
            vmem((4, nx, ny, nz), f32),
            vmem((4, nx, ny, nz), f32),
            vmem((len(stages), 1, nz), f32),
        ]
        + [vmem((total - 1, 1, nz), f32) for total in totals]
        + [sem((2,)), sem((copies,)), sem((copies,)), sem((len(stages),)), sem((len(stages),))],
        compiler_params=pltpu.CompilerParams(
            collective_id=0, has_side_effects=True, vmem_limit_bytes=24 * 1024 * 1024
        ),
        name="substep",
    )(metric, conserved, matter_mask)
    metric_next = metric - (2.0 * step[0, 0]) * curvature
    return metric_next, curvature + curv_add, conserved + fluid_add


def solution(mesh):
    sizes = {axis: mesh.shape[axis] for axis in AXES}
    grid = P(None, "gx", "gy", "gz")
    return jax.shard_map(
        functools.partial(body, sizes),
        mesh=mesh,
        in_specs=(grid, grid, grid, P("gx", "gy", "gz")),
        out_specs=(grid, grid, grid),
        check_vma=False,
    )
```

time: 121 us -> 27.5 us (0.23)
  blocking collectives: 42.2 us -> 0 us
  waiting for transfers between devices: 24.8 us -> 0 us
  local copies, waits for them, and re-layouts: 25.2 us -> 3.79 us
  Pallas kernels: 0 us -> 19.9 us
  other arithmetic: 20.9 us -> 2.18 us
  starting transfers between devices: 5.1 us -> 0 us
    pmax x1 -> x0, blocking collectives: 42.2 us -> none  [body(): speed_max = lax.pmax(local_speed, ('gx', 'gy', 'gz'))]
    ppermute x6 -> x0, waiting for transfers between devices: 24.8 us -> none  [the longest x3 13.8 us: extended(): after = lax.ppermute(first, axis, down)]
    pallas_call x0 -> x1, Pallas kernels: none -> 19.9 us  [body(): pl.pallas_call(functools.partial(kernel, sizes, shape), out_shape=(jax.Sh...]
    slice x7 -> x1, local copies, waits for them, and re-layouts: 12.3 us -> 0.51 us  [body(): metric_next = metric - 2.0 * step[0, 0] * curvature]
    ppermute x4 -> x0, local copies, waits for them, and re-layouts: 8.15 us -> none  [the longest x2 4.12 us: extended(): before = lax.ppermute(last, axis, up)]
    ppermute x6 -> x0, starting transfers between devices: 5.1 us -> none  [the longest x3 4.53 us: extended(): after = lax.ppermute(first, axis, down)]
    mul x8 -> x0, other arithmetic: 3.82 us -> none  [the longest x1 2.5 us: body(): 0.5 * (metric_padded[0:1] + metric_padded[3:4] + metric_padded[5:6])]
    add x2, other arithmetic: 5.69 us -> 2.18 us  [body(): return (metric_next, curvature + curv_add, conserved + fluid_add)]
  transfers between devices with their start and end apart: 6 -> 0, of which waited for: 4 -> 0; matrix products, arithmetic and copies ran while one was open for 9% -> 0% of each run, Pallas kernels for 0% -> 0%
where the time goes in v1:
time: 27.5 us; the launch traced here: 27.2 us
  Pallas kernels  19.9 us (72%)
  local copies, waits for them, and re-layouts  3.79 us (14%)
  other arithmetic  2.18 us (8%)
  between operations  1.31 us (5%)
    pallas_call x1, Pallas kernels, body(): pl.pallas_call(functools.partial(kernel, sizes, shape), out_shape=(jax.Sh...  19.9 us
    unnamed x8, local copies, waits for them, and re-layouts  3.27 us
    add x2, other arithmetic, body(): return (metric_next, curvature + curv_add, conserved + fluid_add)  2.18 us

profile of v1, /device:TPU:0, one launch (start us, length us, event | category | flops | bytes accessed | tf_op | source)
XLA Modules:
  0.0 27.2 jit_solution(4173085388112354863)
XLA Ops:
  0.6 0.0 copy-start
  0.6 1.1 %copy-done = f32[6,16,16,128]{3,2,1,0:T(8,128)S(1)} copy-done((f32[6,16,16,128]{3,2,1,0:T(8,128)S(1)}, f32[6,16,16,128]{3,2,1,0:T(8,128)}, u32[]{:S(2)}) %copy-start) | copy-done | bytes 786456
  1.8 0.0 copy-start.1
  1.8 1.0 %copy-done.1 = f32[4,16,16,128]{3,2,1,0:T(8,128)S(1)} copy-done((f32[4,16,16,128]{3,2,1,0:T(8,128)S(1)}, f32[4,16,16,128]{3,2,1,0:T(8,128)}, u32[]{:S(2)}) %copy-start.1) | copy-done | bytes 524312
  2.8 0.0 copy-start.2
  2.8 0.7 %copy-done.2 = s32[1,1,8]{2,1,0:T(1,128)S(1)} copy-done((s32[1,1,8]{2,1,0:T(1,128)S(1)}, s32[1,1,8]{2,1,0:T(1,128)}, u32[]{:S(2)}) %copy-start.2) | copy-done | bytes 56
  3.5 19.9 %substep.1 = (f32[6,16,16,128]{3,2,1,0:T(8,128)S(1)}, f32[4,16,16,128]{3,2,1,0:T(8,128)S(1)}, f32[8,128]{1,0:T(8,128)S(1)}) custom-call(f32[6,16,16,128]{3,2,1,0:T(8,128)S(1)} %copy-done, f32[4,16,16,128]{3,2,1,0:T(8,128)S(1)} %copy-done.1, s32[1,1,8]{2,1,0:T(1,128)S(1)} %copy-done.2), custom_call_target="tpu_custom_call" | custom-call | tf_op jit(solution)/shard_map/substep/pallas_call | solution.py:312
  23.4 0.5 %slice.3 = f32[1,1]{1,0:T(1,128)} slice(f32[8,128]{1,0:T(8,128)S(1)} %get-tuple-element.6), slice={[0:1], [0:1]} | slice | bytes 8 | tf_op jit(solution)/shard_map/slice | solution.py:344
  24.6 0.0 copy-start.3
  24.6 0.9 %add.7 = f32[4,16,16,128]{3,2,1,0:T(8,128)} add(f32[4,16,16,128]{3,2,1,0:T(8,128)S(1)} %copy-done.1, f32[4,16,16,128]{3,2,1,0:T(8,128)S(1)} %get-tuple-element.8) | non-fusion elementwise | flops 131072 | bytes 1572864 | tf_op jit(solution)/shard_map/add | solution.py:345
  25.5 0.4 %copy-done.3 = f32[6,16,16,128]{3,2,1,0:T(8,128)S(1)} copy-done((f32[6,16,16,128]{3,2,1,0:T(8,128)S(1)}, f32[6,16,16,128]{3,2,1,0:T(8,128)}, u32[]{:S(2)}) %copy-start.3) | copy-done | bytes 786456
  25.9 1.3 %fusion = (f32[6,16,16,128]{3,2,1,0:T(8,128)}, f32[6,16,16,128]{3,2,1,0:T(8,128)}) fusion(f32[6,16,16,128]{3,2,1,0:T(8,128)S(1)} %copy-done.3, f32[6,16,16,128]{3,2,1,0:T(8,128)S(1)} %get-tuple-element.7, f32[6,16,16,128]{3,2,1,0:T(8,128)S(1)} %copy-done, f32[]{:T(128)} %bitcast), kind=kLoop, calls=%fused_computation.1 | loop fusion | flops 589824 | bytes 3932164 | tf_op jit(solution)/shard_map/add | solution.py:345
Async XLA Ops:
  0.6 1.1 %copy-start = (f32[6,16,16,128]{3,2,1,0:T(8,128)S(1)}, f32[6,16,16,128]{3,2,1,0:T(8,128)}, u32[]{:S(2)}) copy-start(f32[6,16,16,128]{3,2,1,0:T(8,128)} %metric_hbm.1) | copy-start | bytes 2359300
  1.8 1.0 %copy-start.1 = (f32[4,16,16,128]{3,2,1,0:T(8,128)S(1)}, f32[4,16,16,128]{3,2,1,0:T(8,128)}, u32[]{:S(2)}) copy-start(f32[4,16,16,128]{3,2,1,0:T(8,128)} %fluid_hbm.1) | copy-start | bytes 1572868
  2.8 0.7 %copy-start.2 = (s32[1,1,8]{2,1,0:T(1,128)S(1)}, s32[1,1,8]{2,1,0:T(1,128)}, u32[]{:S(2)}) copy-start(s32[1,1,8]{2,1,0:T(1,128)} %mask_ref.1) | copy-start | bytes 100
  24.6 1.3 %copy-start.3 = (f32[6,16,16,128]{3,2,1,0:T(8,128)S(1)}, f32[6,16,16,128]{3,2,1,0:T(8,128)}, u32[]{:S(2)}) copy-start(f32[6,16,16,128]{3,2,1,0:T(8,128)} %param.5) | copy-start | bytes 2359300

commit v2 on v1

--- a/solution.py
+++ b/solution.py
@@ -51,8 +51,8 @@
     return flux
 
 
-def kernel(sizes, shape, metric_hbm, fluid_hbm, mask_ref, curv_out, fluid_out, step_out,
-           mp, up, ez, uz, ey, uy, acc_c, acc_f, acc_l, row, *rest):
+def kernel(sizes, shape, metric_hbm, curv_hbm, fluid_hbm, mask_hbm, metric_out, curv_out, fluid_out,
+           mask_ref, cu, mp, up, ez, uz, ey, uy, acc_c, acc_f, acc_l, row, *rest):
     nx, ny, nz = shape
     stages = stages_of(sizes)
     bufs = rest[: len(stages)]
@@ -63,8 +63,12 @@
     own_u = up.at[:, pl.ds(1, nx)]
     load_u = pltpu.make_async_copy(fluid_hbm, own_u, load_sem.at[0])
     load_m = pltpu.make_async_copy(metric_hbm, own_m, load_sem.at[1])
+    load_mask = pltpu.make_async_copy(mask_hbm, mask_ref, load_sem.at[2])
+    load_c = pltpu.make_async_copy(curv_hbm, cu, load_sem.at[3])
+    load_mask.start()
     load_u.start()
     load_m.start()
+    load_c.start()
 
     barrier = pltpu.get_barrier_semaphore()
     greeted = 0
@@ -78,6 +82,7 @@
         lax.fori_loop(1, total, greet, 0)
         greeted += total - 1
 
+    load_mask.wait()
     lane = lax.broadcasted_iota(jnp.int32, (ny, nz), 1)
     block = lane // MB
     mask = jnp.zeros((ny, nz), jnp.int32)
@@ -249,9 +254,17 @@
         best = gathered(index, best)
     speed_max = jnp.max(best, axis=1, keepdims=True)
     step = courant / speed_max
-    step_out[...] = jnp.broadcast_to(step, step_out.shape)
     step_all = jnp.broadcast_to(step, (ny, nz))
     half_speed = jnp.broadcast_to(0.5 * speed_max, (ny, nz))
+
+    load_c.wait()
+
+    def advance_metric(x, carry):
+        for c in range(6):
+            metric_out[c, x] = mp[c, x + W] - (2.0 * step_all) * cu[c, x]
+        return carry
+
+    lax.fori_loop(0, nx, advance_metric, 0)
 
     for copy in y_copies:
         copy.wait()
@@ -279,7 +292,7 @@
                 total = total + weight[k] * near
                 if c in trace_part:
                     grad = grad + slope[k] * near
-            curv_out[c, x] = step_all * (acc_c[c, x] - 0.5 * placed(total))
+            curv_out[c, x] = cu[c, x] + step_all * (acc_c[c, x] - 0.5 * placed(total))
         halo = [uy[c, x] for c in range(4)]
         flux = flux_of(halo, 1)
         density = up[0, x + 1]
@@ -293,7 +306,8 @@
             if c == 2:
                 value = value + (0.5 * density) * placed(grad)
             value = step_all * (value + half_speed * (acc_l[c, x] + near))
-            fluid_out[c, x] = jnp.where(mask, value, 0.0)
+            own = up[c, x + 1]
+            fluid_out[c, x] = jnp.where(mask, own + value, own)
         return carry
 
     lax.fori_loop(0, nx, finish, 0)
@@ -309,20 +323,18 @@
     copies = 8 + 2 * sides
     vmem, sem = pltpu.VMEM, pltpu.SemaphoreType.DMA
     f32 = jnp.float32
-    curv_add, fluid_add, step = pl.pallas_call(
+    return pl.pallas_call(
         functools.partial(kernel, sizes, shape),
         out_shape=(
             jax.ShapeDtypeStruct((6,) + shape, f32),
+            jax.ShapeDtypeStruct((6,) + shape, f32),
             jax.ShapeDtypeStruct((4,) + shape, f32),
-            jax.ShapeDtypeStruct((SUB, nz), f32),
         ),
-        in_specs=[
-            pl.BlockSpec(memory_space=pl.ANY),
-            pl.BlockSpec(memory_space=pl.ANY),
-            pl.BlockSpec(memory_space=pltpu.SMEM),
-        ],
+        in_specs=[pl.BlockSpec(memory_space=pltpu.HBM)] * 4,
         out_specs=(pl.BlockSpec(memory_space=vmem),) * 3,
         scratch_shapes=[
+            pltpu.SMEM(matter_mask.shape, jnp.int32),
+            vmem((6, nx, ny, nz), f32),
             vmem((6, nx + 2 * W, ny, nz), f32),
             vmem((4, nx + 2, ny, nz), f32),
             vmem((sides, 6, nx, ny, nz), f32),
@@ -335,14 +347,12 @@
             vmem((len(stages), 1, nz), f32),
         ]
         + [vmem((total - 1, 1, nz), f32) for total in totals]
-        + [sem((2,)), sem((copies,)), sem((copies,)), sem((len(stages),)), sem((len(stages),))],
+        + [sem((4,)), sem((copies,)), sem((copies,)), sem((len(stages),)), sem((len(stages),))],
         compiler_params=pltpu.CompilerParams(
             collective_id=0, has_side_effects=True, vmem_limit_bytes=24 * 1024 * 1024
         ),
         name="substep",
-    )(metric, conserved, matter_mask)
-    metric_next = metric - (2.0 * step[0, 0]) * curvature
-    return metric_next, curvature + curv_add, conserved + fluid_add
+    )(metric, curvature, conserved, matter_mask)
 
 
 def solution(mesh):

time: 27.5 us -> 27.1 us (0.985)
  local copies, waits for them, and re-layouts: 3.79 us -> 6.51 us
  other arithmetic: 2.18 us -> 0 us
  between operations: 1.31 us -> 0.65 us
  Pallas kernels: 19.9 us -> 19.6 us
    unnamed x8 -> x11, local copies, waits for them, and re-layouts: 3.27 us -> 6.51 us
    add x2 -> x0, other arithmetic: 2.18 us -> none  [body(): return (metric_next, curvature + curv_add, conserved + fluid_add)]
    slice x1 -> x0, local copies, waits for them, and re-layouts: 0.51 us -> none  [body(): metric_next = metric - 2.0 * step[0, 0] * curvature]
    pallas_call x1, Pallas kernels: 19.9 us -> 19.6 us  [body(): pl.pallas_call(functools.partial(kernel, sizes, shape), out_shape=(jax.Sh...]
where the time goes in v2:
time: 27.1 us; the launch traced here: 26.8 us
  Pallas kernels  19.6 us (72%)
  local copies, waits for them, and re-layouts  6.51 us (24%)
  between operations  0.65 us (2%)
    pallas_call x1, Pallas kernels, body(): pl.pallas_call(functools.partial(kernel, sizes, shape), out_shape=(jax.Sh...  19.6 us
    unnamed x11, local copies, waits for them, and re-layouts  6.51 us

profile of v2, /device:TPU:0, one launch (start us, length us, event | category | flops | bytes accessed | tf_op | source)
XLA Modules:
  0.0 26.8 jit_solution(4361002747349649999)
XLA Ops:
  0.6 0.0 copy-start
  0.6 1.1 %copy-done = f32[6,16,16,128]{3,2,1,0:T(8,128)S(1)} copy-done((f32[6,16,16,128]{3,2,1,0:T(8,128)S(1)}, f32[6,16,16,128]{3,2,1,0:T(8,128)}, u32[]{:S(2)}) %copy-start) | copy-done | bytes 786456
  1.8 0.0 copy-start.1
  1.8 1.1 %copy-done.1 = f32[6,16,16,128]{3,2,1,0:T(8,128)S(1)} copy-done((f32[6,16,16,128]{3,2,1,0:T(8,128)S(1)}, f32[6,16,16,128]{3,2,1,0:T(8,128)}, u32[]{:S(2)}) %copy-start.1) | copy-done | bytes 786456
  2.9 0.0 copy-start.2
  2.9 1.0 %copy-done.2 = f32[4,16,16,128]{3,2,1,0:T(8,128)S(1)} copy-done((f32[4,16,16,128]{3,2,1,0:T(8,128)S(1)}, f32[4,16,16,128]{3,2,1,0:T(8,128)}, u32[]{:S(2)}) %copy-start.2) | copy-done | bytes 524312
  3.9 0.0 copy-start.3
  3.9 0.7 %copy-done.3 = s32[1,1,8]{2,1,0:T(1,128)S(1)} copy-done((s32[1,1,8]{2,1,0:T(1,128)S(1)}, s32[1,1,8]{2,1,0:T(1,128)}, u32[]{:S(2)}) %copy-start.3) | copy-done | bytes 56
  4.6 19.6 %substep.1 = (f32[6,16,16,128]{3,2,1,0:T(8,128)S(1)}, f32[6,16,16,128]{3,2,1,0:T(8,128)S(1)}, f32[4,16,16,128]{3,2,1,0:T(8,128)S(1)}) custom-call(f32[6,16,16,128]{3,2,1,0:T(8,128)S(1)} %copy-done, f32[6,16,16,128]{3,2,1,0:T(8,128)S(1)} %copy-done.1, f32[4,16,16,128]{3,2,1,0:T(8,128)S(1)} %copy-done.2, s32[1,1,8]{2,1,0:T(1,128)S(1)} %copy-done.3), custom_call_target="tpu_custom_call" | custom-call | tf_op jit(solution)/shard_map/substep/pallas_call | solution.py:326
  24.2 0.9 %copy.10 = f32[6,16,16,128]{3,2,1,0:T(8,128)} copy(f32[6,16,16,128]{3,2,1,0:T(8,128)S(1)} %get-tuple-element.6) | data formatting | bytes 1572864
  25.1 0.9 %copy.11 = f32[6,16,16,128]{3,2,1,0:T(8,128)} copy(f32[6,16,16,128]{3,2,1,0:T(8,128)S(1)} %get-tuple-element.7) | data formatting | bytes 1572864
  26.0 0.8 %copy.12 = f32[4,16,16,128]{3,2,1,0:T(8,128)} copy(f32[4,16,16,128]{3,2,1,0:T(8,128)S(1)} %get-tuple-element.8) | data formatting | bytes 1048576
Async XLA Ops:
  0.6 1.1 %copy-start = (f32[6,16,16,128]{3,2,1,0:T(8,128)S(1)}, f32[6,16,16,128]{3,2,1,0:T(8,128)}, u32[]{:S(2)}) copy-start(f32[6,16,16,128]{3,2,1,0:T(8,128)} %metric_hbm.1) | copy-start | bytes 2359300
  1.8 1.1 %copy-start.1 = (f32[6,16,16,128]{3,2,1,0:T(8,128)S(1)}, f32[6,16,16,128]{3,2,1,0:T(8,128)}, u32[]{:S(2)}) copy-start(f32[6,16,16,128]{3,2,1,0:T(8,128)} %curv_hbm.1) | copy-start | bytes 2359300
  2.9 1.0 %copy-start.2 = (f32[4,16,16,128]{3,2,1,0:T(8,128)S(1)}, f32[4,16,16,128]{3,2,1,0:T(8,128)}, u32[]{:S(2)}) copy-start(f32[4,16,16,128]{3,2,1,0:T(8,128)} %fluid_hbm.1) | copy-start | bytes 1572868
  3.9 0.7 %copy-start.3 = (s32[1,1,8]{2,1,0:T(1,128)S(1)}, s32[1,1,8]{2,1,0:T(1,128)}, u32[]{:S(2)}) copy-start(s32[1,1,8]{2,1,0:T(1,128)} %mask_hbm.1) | copy-start | bytes 100

commit v3 on v2

--- a/solution.py
+++ b/solution.py
@@ -313,6 +313,15 @@
     lax.fori_loop(0, nx, finish, 0)
 
 
+def store(*refs):
+    sems = refs[-1]
+    copies = [pltpu.make_async_copy(refs[i], refs[3 + i], sems.at[i]) for i in range(3)]
+    for copy in copies:
+        copy.start()
+    for copy in copies:
+        copy.wait()
+
+
 def body(sizes, metric, curvature, conserved, matter_mask):
     shape = metric.shape[1:]
     nx, ny, nz = shape
@@ -323,12 +332,15 @@
     copies = 8 + 2 * sides
     vmem, sem = pltpu.VMEM, pltpu.SemaphoreType.DMA
     f32 = jnp.float32
-    return pl.pallas_call(
+    metric, curvature, conserved, matter_mask = [
+        pltpu.with_memory_space_constraint(x, pltpu.HBM) for x in (metric, curvature, conserved, matter_mask)
+    ]
+    parts = pl.pallas_call(
         functools.partial(kernel, sizes, shape),
         out_shape=(
-            jax.ShapeDtypeStruct((6,) + shape, f32),
-            jax.ShapeDtypeStruct((6,) + shape, f32),
-            jax.ShapeDtypeStruct((4,) + shape, f32),
+            vmem((6,) + shape, f32),
+            vmem((6,) + shape, f32),
+            vmem((4,) + shape, f32),
         ),
         in_specs=[pl.BlockSpec(memory_space=pltpu.HBM)] * 4,
         out_specs=(pl.BlockSpec(memory_space=vmem),) * 3,
@@ -353,6 +365,15 @@
         ),
         name="substep",
     )(metric, curvature, conserved, matter_mask)
+    return pl.pallas_call(
+        store,
+        out_shape=tuple(jax.ShapeDtypeStruct(part.shape, f32) for part in parts),
+        in_specs=[pl.BlockSpec(memory_space=vmem)] * 3,
+        out_specs=(pl.BlockSpec(memory_space=pl.ANY),) * 3,
+        scratch_shapes=[sem((3,))],
+        compiler_params=pltpu.CompilerParams(vmem_limit_bytes=1024 * 1024),
+        name="store",
+    )(*parts)
 
 
 def solution(mesh):

time: 27.1 us -> 21.6 us (0.80)
  local copies, waits for them, and re-layouts: 6.51 us -> 0 us
  Pallas kernels: 19.6 us -> 20.8 us
    unnamed x11 -> x0, local copies, waits for them, and re-layouts: 6.51 us -> none
    pallas_call x1 -> x2, Pallas kernels: 19.6 us -> 20.8 us  [the longest x1 19.5 us: body(): pl.pallas_call(functools.partial(kernel, sizes, shape), out_shape=(vmem((...]
where the time goes in v3:
time: 21.6 us; the launch traced here: 21.5 us
  Pallas kernels  20.8 us (96%)
  between operations  0.64 us (3%)
    pallas_call x1, Pallas kernels, body(): pl.pallas_call(functools.partial(kernel, sizes, shape), out_shape=(vmem((...  19.5 us
    pallas_call x1, Pallas kernels, body(): pl.pallas_call(store, out_shape=tuple((jax.ShapeDtypeStruct(part.shape, f...  1.34 us

profile of v3, /device:TPU:0, one launch (start us, length us, event | category | flops | bytes accessed | tf_op | source)
XLA Modules:
  0.0 21.5 jit_solution(13611489725159024164)
XLA Ops:
  0.6 19.5 %substep.1 = (f32[6,16,16,128]{3,2,1,0:T(8,128)S(1)}, f32[6,16,16,128]{3,2,1,0:T(8,128)S(1)}, f32[4,16,16,128]{3,2,1,0:T(8,128)S(1)}) custom-call(f32[6,16,16,128]{3,2,1,0:T(8,128)} %metric_hbm.1, f32[6,16,16,128]{3,2,1,0:T(8,128)} %curv_hbm.1, f32[4,16,16,128]{3,2,1,0:T(8,128)} %fluid_hbm.1, s32[1,1,8]{2,1,0:T(1,128)} %mask_hbm.1), custom_call_target="tpu_custom_call" | custom-call | tf_op jit(solution)/shard_map/substep/pallas_call | solution.py:338
  20.1 1.3 %store.1 = (f32[6,16,16,128]{3,2,1,0:T(8,128)}, f32[6,16,16,128]{3,2,1,0:T(8,128)}, f32[4,16,16,128]{3,2,1,0:T(8,128)}) custom-call(f32[6,16,16,128]{3,2,1,0:T(8,128)S(1)} %get-tuple-element.6.refs_0_, f32[6,16,16,128]{3,2,1,0:T(8,128)S(1)} %get-tuple-element.7.refs_1_, f32[4,16,16,128]{3,2,1,0:T(8,128)S(1)} %get-tuple-element.8.refs_2_), custom_call_target="tpu_custom_call" | custom-call | tf_op jit(solution)/shard_map/store/pallas_call | solution.py:368

commit v4 on v3

--- a/solution.py
+++ b/solution.py
@@ -65,22 +65,22 @@
     load_m = pltpu.make_async_copy(metric_hbm, own_m, load_sem.at[1])
     load_mask = pltpu.make_async_copy(mask_hbm, mask_ref, load_sem.at[2])
     load_c = pltpu.make_async_copy(curv_hbm, cu, load_sem.at[3])
+    barrier = pltpu.get_barrier_semaphore()
+    greeted = 0
+    for axes in stages:
+        total = math.prod(sizes[axis] for axis in axes)
+
+        def greet(j, carry, axes=axes):
+            pl.semaphore_signal(barrier, inc=1, device_id=peer(sizes, axes, j), device_id_type=MESH)
+            return carry
+
+        lax.fori_loop(1, total, greet, 0)
+        greeted += total - 1
+
     load_mask.start()
     load_u.start()
     load_m.start()
     load_c.start()
-
-    barrier = pltpu.get_barrier_semaphore()
-    greeted = 0
-    for axes in stages:
-        total = math.prod(sizes[axis] for axis in axes)
-
-        def greet(j, carry, axes=axes):
-            pl.semaphore_signal(barrier, inc=1, device_id=peer(sizes, axes, j), device_id_type=MESH)
-            return carry
-
-        lax.fori_loop(1, total, greet, 0)
-        greeted += total - 1
 
     load_mask.wait()
     lane = lax.broadcasted_iota(jnp.int32, (ny, nz), 1)
@@ -122,8 +122,6 @@
         pltpu.make_async_copy(buf, buf, row_recv.at[index]).wait()
         pltpu.make_async_copy(buf, buf, row_send.at[index]).wait()
         return jnp.maximum(best, jnp.max(buf[...], axis=0))
-
-    spread(0)
 
     count = [0]
 
@@ -137,21 +135,27 @@
         copy.start()
         return copy
 
-    y_copies = [
-        remote(mp.at[:, pl.ds(W, nx), pl.ds(ny - W, W)], ey.at[:, :, pl.ds(SUB - W, W)], "gy", 1),
-        remote(mp.at[:, pl.ds(W, nx), pl.ds(0, W)], ey.at[:, :, pl.ds(0, W)], "gy", -1),
-        remote(up.at[:, pl.ds(1, nx), pl.ds(ny - 1, 1)], uy.at[:, :, pl.ds(SUB - 1, 1)], "gy", 1),
-        remote(up.at[:, pl.ds(1, nx), pl.ds(0, 1)], uy.at[:, :, pl.ds(0, 1)], "gy", -1),
-    ]
-    x_copies = [
-        remote(mp.at[:, pl.ds(nx, W)], mp.at[:, pl.ds(0, W)], "gx", 1),
-        remote(mp.at[:, pl.ds(W, W)], mp.at[:, pl.ds(nx + W, W)], "gx", -1),
-        remote(up.at[:, pl.ds(nx, 1)], up.at[:, pl.ds(0, 1)], "gx", 1),
-        remote(up.at[:, pl.ds(1, 1)], up.at[:, pl.ds(nx + 1, 1)], "gx", -1),
-    ]
     z_copies = [remote(own_u, uz.at[0], "gz", -1), remote(own_m, ez.at[0], "gz", -1)]
     if sizes["gz"] > 2:
         z_copies += [remote(own_u, uz.at[1], "gz", 1), remote(own_m, ez.at[1], "gz", 1)]
+
+    def metric_sides(start):
+        some = pl.ds(start, 3)
+        return [
+            remote(mp.at[some, pl.ds(W, nx), pl.ds(ny - W, W)], ey.at[some, :, pl.ds(SUB - W, W)], "gy", 1),
+            remote(mp.at[some, pl.ds(W, nx), pl.ds(0, W)], ey.at[some, :, pl.ds(0, W)], "gy", -1),
+            remote(mp.at[some, pl.ds(nx, W)], mp.at[some, pl.ds(0, W)], "gx", 1),
+            remote(mp.at[some, pl.ds(W, W)], mp.at[some, pl.ds(nx + W, W)], "gx", -1),
+        ]
+
+    early = [
+        remote(up.at[:, pl.ds(1, nx), pl.ds(ny - 1, 1)], uy.at[:, :, pl.ds(SUB - 1, 1)], "gy", 1),
+        remote(up.at[:, pl.ds(1, nx), pl.ds(0, 1)], uy.at[:, :, pl.ds(0, 1)], "gy", -1),
+        remote(up.at[:, pl.ds(nx, 1)], up.at[:, pl.ds(0, 1)], "gx", 1),
+        remote(up.at[:, pl.ds(1, 1)], up.at[:, pl.ds(nx + 1, 1)], "gx", -1),
+    ] + metric_sides(0)
+    spread(0)
+    late = metric_sides(3)
 
     def edge(ref, c, x):
         if sizes["gz"] > 2:
@@ -221,31 +225,64 @@
 
     lax.fori_loop(0, nx, inner, 0)
 
-    for copy in x_copies:
+    inside = jnp.logical_and(sub >= W, sub < SUB - W)
+    weight, slope = [None], [None]
+    for k in range(1, W + 1):
+        touched = jnp.where(jnp.logical_or(sub < k, sub >= SUB - k), 1.0, 0.0)
+        weight.append(touched * jnp.float32(second[k]))
+        slope.append(jnp.where(sub < SUB // 2, -1.0, 1.0) * touched * jnp.float32(first[k]))
+    low_half = sub < SUB // 2
+    nothing = jnp.zeros((SUB, nz), jnp.float32)
+
+    def placed(value):
+        parts = [jnp.where(low_half, value, nothing)] + [nothing] * (tiles - 2) + [jnp.where(low_half, nothing, value)]
+        return jnp.concatenate(parts, axis=0)
+
+    def sides(c, x):
+        total = jnp.zeros((ny, nz), jnp.float32)
+        grad_x = jnp.zeros((ny, nz), jnp.float32)
+        halo = jnp.where(inside, nothing, ey[c, x])
+        rows, grad_y = nothing, nothing
+        for k in range(1, W + 1):
+            high, low = mp[c, x + W + k], mp[c, x + W - k]
+            near = jnp.where(low_half, pltpu.roll(halo, k, 0), pltpu.roll(halo, SUB - k, 0))
+            total = total + second[k] * (high + low)
+            rows = rows + weight[k] * near
+            grad_x = grad_x + first[k] * (high - low)
+            grad_y = grad_y + slope[k] * near
+        return total + placed(rows), grad_x, grad_y
+
+    for copy in early:
         copy.wait()
 
-    def along_x(x, carry):
+    def first_half(x, carry):
+        for c in range(3):
+            total, grad_x, grad_y = sides(c, x)
+            acc_c[c, x] = acc_c[c, x] - 0.5 * total
+            if c == 0:
+                gx, gy = grad_x, placed(grad_y)
+        half_density = 0.5 * up[0, x + 1]
         above = [up[c, x + 2] for c in range(4)]
         below = [up[c, x] for c in range(4)]
         flux_above, flux_below = flux_of(above, 0), flux_of(below, 0)
-        grad = jnp.zeros((ny, nz), jnp.float32)
-        for c in range(6):
-            total = jnp.zeros((ny, nz), jnp.float32)
-            for k in range(1, W + 1):
-                high, low = mp[c, x + W + k], mp[c, x + W - k]
-                total = total + second[k] * (high + low)
-                if c in trace_part:
-                    grad = grad + first[k] * (high - low)
-            acc_c[c, x] = acc_c[c, x] - 0.5 * total
+        halo = [uy[c, x] for c in range(4)]
+        flux = flux_of(halo, 1)
+        end = jnp.logical_or(sub == 0, sub == SUB - 1)
         for c in range(4):
-            value = acc_f[c, x] - 0.5 * (flux_above[c] - flux_below[c])
+            near = jnp.where(sub == 0, pltpu.roll(halo[c], 1, 0), pltpu.roll(halo[c], SUB - 1, 0))
+            near_flux = jnp.where(sub == 0, -pltpu.roll(flux[c], 1, 0), pltpu.roll(flux[c], SUB - 1, 0))
+            near = placed(jnp.where(end, near, nothing))
+            near_flux = placed(jnp.where(end, near_flux, nothing))
+            value = acc_f[c, x] - 0.5 * ((flux_above[c] - flux_below[c]) + near_flux)
             if c == 1:
-                value = value + (0.5 * up[0, x + 1]) * grad
+                value = value + half_density * gx
+            if c == 2:
+                value = value + half_density * gy
             acc_f[c, x] = value
-            acc_l[c, x] = acc_l[c, x] + (above[c] + below[c])
+            acc_l[c, x] = acc_l[c, x] + ((above[c] + below[c]) + near)
         return carry
 
-    lax.fori_loop(0, nx, along_x, 0)
+    lax.fori_loop(0, nx, first_half, 0)
 
     best = gathered(0, best)
     for index in range(1, len(stages)):
@@ -259,58 +296,38 @@
 
     load_c.wait()
 
-    def advance_metric(x, carry):
+    def advance(x, carry):
         for c in range(6):
             metric_out[c, x] = mp[c, x + W] - (2.0 * step_all) * cu[c, x]
+        for c in range(3):
+            curv_out[c, x] = cu[c, x] + step_all * acc_c[c, x]
+        own = [up[c, x + 1] for c in range(4)]
+        for c in (0, 3):
+            add = acc_f[c, x] + half_speed * acc_l[c, x]
+            fluid_out[c, x] = jnp.where(mask, own[c] + step_all * add, own[c])
         return carry
 
-    lax.fori_loop(0, nx, advance_metric, 0)
-
-    for copy in y_copies:
+    lax.fori_loop(0, nx, advance, 0)
+
+    for copy in late:
         copy.wait()
 
-    inside = jnp.logical_and(sub >= W, sub < SUB - W)
-    weight, slope = [None], [None]
-    for k in range(1, W + 1):
-        touched = jnp.where(jnp.logical_or(sub < k, sub >= SUB - k), 1.0, 0.0)
-        weight.append(touched * jnp.float32(second[k]))
-        slope.append(jnp.where(sub < SUB // 2, -1.0, 1.0) * touched * jnp.float32(first[k]))
-    low_half = sub < SUB // 2
-    nothing = jnp.zeros((SUB, nz), jnp.float32)
-
-    def placed(value):
-        parts = [jnp.where(low_half, value, nothing)] + [nothing] * (tiles - 2) + [jnp.where(low_half, nothing, value)]
-        return jnp.concatenate(parts, axis=0)
-
-    def finish(x, carry):
-        grad = nothing
-        for c in range(6):
-            halo = jnp.where(inside, nothing, ey[c, x])
-            total = nothing
-            for k in range(1, W + 1):
-                near = jnp.where(low_half, pltpu.roll(halo, k, 0), pltpu.roll(halo, SUB - k, 0))
-                total = total + weight[k] * near
-                if c in trace_part:
-                    grad = grad + slope[k] * near
-            curv_out[c, x] = cu[c, x] + step_all * (acc_c[c, x] - 0.5 * placed(total))
-        halo = [uy[c, x] for c in range(4)]
-        flux = flux_of(halo, 1)
-        density = up[0, x + 1]
-        for c in range(4):
-            near = jnp.where(sub == 0, pltpu.roll(halo[c], 1, 0), pltpu.roll(halo[c], SUB - 1, 0))
-            near_flux = jnp.where(sub == 0, -pltpu.roll(flux[c], 1, 0), pltpu.roll(flux[c], SUB - 1, 0))
-            end = jnp.logical_or(sub == 0, sub == SUB - 1)
-            near = placed(jnp.where(end, near, nothing))
-            near_flux = placed(jnp.where(end, near_flux, nothing))
-            value = acc_f[c, x] - 0.5 * near_flux
-            if c == 2:
-                value = value + (0.5 * density) * placed(grad)
-            value = step_all * (value + half_speed * (acc_l[c, x] + near))
+    def second_half(x, carry):
+        gx = jnp.zeros((ny, nz), jnp.float32)
+        gy = nothing
+        for c in range(3, 6):
+            total, grad_x, grad_y = sides(c, x)
+            curv_out[c, x] = cu[c, x] + step_all * (acc_c[c, x] - 0.5 * total)
+            if c in trace_part:
+                gx, gy = gx + grad_x, gy + grad_y
+        half_density = 0.5 * up[0, x + 1]
+        for c, grad in ((1, gx), (2, placed(gy))):
             own = up[c, x + 1]
-            fluid_out[c, x] = jnp.where(mask, own + value, own)
+            add = acc_f[c, x] + half_density * grad + half_speed * acc_l[c, x]
+            fluid_out[c, x] = jnp.where(mask, own + step_all * add, own)
         return carry
 
-    lax.fori_loop(0, nx, finish, 0)
+    lax.fori_loop(0, nx, second_half, 0)
 
 
 def store(*refs):
@@ -329,7 +346,7 @@
     stages = stages_of(sizes)
     totals = [math.prod(sizes[axis] for axis in axes) for axes in stages]
     sides = 2 if sizes["gz"] > 2 else 1
-    copies = 8 + 2 * sides
+    copies = 12 + 2 * sides
     vmem, sem = pltpu.VMEM, pltpu.SemaphoreType.DMA
     f32 = jnp.float32
     metric, curvature, conserved, matter_mask = [

time: 21.6 us -> 19.9 us (0.921)
  Pallas kernels: 20.8 us -> 19.1 us
    pallas_call x1, Pallas kernels: 19.5 us -> 17.8 us  [body(): pl.pallas_call(functools.partial(kernel, sizes, shape), out_shape=(vmem((...]
where the time goes in v4:
time: 19.9 us; the launch traced here: 19.7 us
  Pallas kernels  19.1 us (96%)
  between operations  0.64 us (3%)
    pallas_call x1, Pallas kernels, body(): pl.pallas_call(functools.partial(kernel, sizes, shape), out_shape=(vmem((...  17.8 us
    pallas_call x1, Pallas kernels, body(): pl.pallas_call(store, out_shape=tuple((jax.ShapeDtypeStruct(part.shape, f...  1.34 us

profile of v4, /device:TPU:0, one launch (start us, length us, event | category | flops | bytes accessed | tf_op | source)
XLA Modules:
  0.0 19.7 jit_solution(11695584611549997386)
XLA Ops:
  0.6 17.8 %substep.1 = (f32[6,16,16,128]{3,2,1,0:T(8,128)S(1)}, f32[6,16,16,128]{3,2,1,0:T(8,128)S(1)}, f32[4,16,16,128]{3,2,1,0:T(8,128)S(1)}) custom-call(f32[6,16,16,128]{3,2,1,0:T(8,128)} %metric_hbm.1, f32[6,16,16,128]{3,2,1,0:T(8,128)} %curv_hbm.1, f32[4,16,16,128]{3,2,1,0:T(8,128)} %fluid_hbm.1, s32[1,1,8]{2,1,0:T(1,128)} %mask_hbm.1), custom_call_target="tpu_custom_call" | custom-call | tf_op jit(solution)/shard_map/substep/pallas_call | solution.py:355
  18.4 1.3 %store.1 = (f32[6,16,16,128]{3,2,1,0:T(8,128)}, f32[6,16,16,128]{3,2,1,0:T(8,128)}, f32[4,16,16,128]{3,2,1,0:T(8,128)}) custom-call(f32[6,16,16,128]{3,2,1,0:T(8,128)S(1)} %get-tuple-element.6.refs_0_, f32[6,16,16,128]{3,2,1,0:T(8,128)S(1)} %get-tuple-element.7.refs_1_, f32[4,16,16,128]{3,2,1,0:T(8,128)S(1)} %get-tuple-element.8.refs_2_), custom_call_target="tpu_custom_call" | custom-call | tf_op jit(solution)/shard_map/store/pallas_call | solution.py:385

commit v5 on v4

--- a/solution.py
+++ b/solution.py
@@ -22,6 +22,7 @@
 trace_part = (0, 3, 5)
 W = 3
 SUB = 8
+EARLY = 4
 
 
 def peer(sizes, axes, offset):
@@ -139,8 +140,8 @@
     if sizes["gz"] > 2:
         z_copies += [remote(own_u, uz.at[1], "gz", 1), remote(own_m, ez.at[1], "gz", 1)]
 
-    def metric_sides(start):
-        some = pl.ds(start, 3)
+    def metric_sides(start, stop):
+        some = pl.ds(start, stop - start)
         return [
             remote(mp.at[some, pl.ds(W, nx), pl.ds(ny - W, W)], ey.at[some, :, pl.ds(SUB - W, W)], "gy", 1),
             remote(mp.at[some, pl.ds(W, nx), pl.ds(0, W)], ey.at[some, :, pl.ds(0, W)], "gy", -1),
@@ -153,9 +154,9 @@
         remote(up.at[:, pl.ds(1, nx), pl.ds(0, 1)], uy.at[:, :, pl.ds(0, 1)], "gy", -1),
         remote(up.at[:, pl.ds(nx, 1)], up.at[:, pl.ds(0, 1)], "gx", 1),
         remote(up.at[:, pl.ds(1, 1)], up.at[:, pl.ds(nx + 1, 1)], "gx", -1),
-    ] + metric_sides(0)
+    ] + metric_sides(0, EARLY)
     spread(0)
-    late = metric_sides(3)
+    late = metric_sides(EARLY, 6)
 
     def edge(ref, c, x):
         if sizes["gz"] > 2:
@@ -256,11 +257,13 @@
         copy.wait()
 
     def first_half(x, carry):
-        for c in range(3):
+        gx, gy = jnp.zeros((ny, nz), jnp.float32), nothing
+        for c in range(EARLY):
             total, grad_x, grad_y = sides(c, x)
             acc_c[c, x] = acc_c[c, x] - 0.5 * total
-            if c == 0:
-                gx, gy = grad_x, placed(grad_y)
+            if c in trace_part:
+                gx, gy = gx + grad_x, gy + grad_y
+        gy = placed(gy)
         half_density = 0.5 * up[0, x + 1]
         above = [up[c, x + 2] for c in range(4)]
         below = [up[c, x] for c in range(4)]
@@ -299,7 +302,7 @@
     def advance(x, carry):
         for c in range(6):
             metric_out[c, x] = mp[c, x + W] - (2.0 * step_all) * cu[c, x]
-        for c in range(3):
+        for c in range(EARLY):
             curv_out[c, x] = cu[c, x] + step_all * acc_c[c, x]
         own = [up[c, x + 1] for c in range(4)]
         for c in (0, 3):
@@ -315,7 +318,7 @@
     def second_half(x, carry):
         gx = jnp.zeros((ny, nz), jnp.float32)
         gy = nothing
-        for c in range(3, 6):
+        for c in range(EARLY, 6):
             total, grad_x, grad_y = sides(c, x)
             curv_out[c, x] = cu[c, x] + step_all * (acc_c[c, x] - 0.5 * total)
             if c in trace_part:
@@ -327,7 +330,7 @@
             fluid_out[c, x] = jnp.where(mask, own + step_all * add, own)
         return carry
 
-    lax.fori_loop(0, nx, second_half, 0)
+    lax.fori_loop(0, nx, second_half, 0, unroll=2)
 
 
 def store(*refs):

time: 19.9 us -> 19.8 us (level)
  no operation moved by 1% of the time
where the time goes in v5:
time: 19.8 us; the launch traced here: 19.7 us
  Pallas kernels  19 us (96%)
  between operations  0.64 us (3%)
    pallas_call x1, Pallas kernels, body(): pl.pallas_call(functools.partial(kernel, sizes, shape), out_shape=(vmem((...  17.7 us
    pallas_call x1, Pallas kernels, body(): pl.pallas_call(store, out_shape=tuple((jax.ShapeDtypeStruct(part.shape, f...  1.34 us

profile of v5, /device:TPU:0, one launch (start us, length us, event | category | flops | bytes accessed | tf_op | source)
XLA Modules:
  0.0 19.7 jit_solution(7361490672880187444)
XLA Ops:
  0.6 17.7 %substep.1 = (f32[6,16,16,128]{3,2,1,0:T(8,128)S(1)}, f32[6,16,16,128]{3,2,1,0:T(8,128)S(1)}, f32[4,16,16,128]{3,2,1,0:T(8,128)S(1)}) custom-call(f32[6,16,16,128]{3,2,1,0:T(8,128)} %metric_hbm.1, f32[6,16,16,128]{3,2,1,0:T(8,128)} %curv_hbm.1, f32[4,16,16,128]{3,2,1,0:T(8,128)} %fluid_hbm.1, s32[1,1,8]{2,1,0:T(1,128)} %mask_hbm.1), custom_call_target="tpu_custom_call" | custom-call | tf_op jit(solution)/shard_map/substep/pallas_call | solution.py:358
  18.3 1.3 %store.1 = (f32[6,16,16,128]{3,2,1,0:T(8,128)}, f32[6,16,16,128]{3,2,1,0:T(8,128)}, f32[4,16,16,128]{3,2,1,0:T(8,128)}) custom-call(f32[6,16,16,128]{3,2,1,0:T(8,128)S(1)} %get-tuple-element.6.refs_0_, f32[6,16,16,128]{3,2,1,0:T(8,128)S(1)} %get-tuple-element.7.refs_1_, f32[4,16,16,128]{3,2,1,0:T(8,128)S(1)} %get-tuple-element.8.refs_2_), custom_call_target="tpu_custom_call" | custom-call | tf_op jit(solution)/shard_map/store/pallas_call | solution.py:388
